TPU v7x, 512 devices: a 4x2x32 block of a 4x8x32 slice. The times are simulated.
512 devices in a mesh: member: 2 (over y), tile: 32 (over z), row: 4 (over x), lev: 2 (over core).
Axes of the slice: x: 4, y: 2, z: 32, core: 2. Of those that a mesh axis runs over, the one named last changes fastest.
The devices are a block of a 4x8x32 slice.
Arguments:
- thickness: float32 [128, 512, 512], P(('member', 'lev'), 'tile', 'row'), parts along dimension 0, may hold values from 0.24 to 14.91
- zonal_wind: float32 [128, 512, 512], P(('member', 'lev'), 'tile', 'row'), parts along dimension 0, may hold values from -1.8 to 1.8
- merid_wind: float32 [128, 512, 512], P(('member', 'lev'), 'tile', 'row'), parts along dimension 0, may hold values from -1.8 to 1.8
- pert_codes: int32 [1024, 512], P(('member', 'tile'), 'row'), parts along dimension 0, may hold values from 0 to 1073741823
Outputs:
- thick_out: float32 [128, 512, 512], P(('member', 'lev'), 'tile', 'row'), parts along dimension 0
- zonal_out: float32 [128, 512, 512], P(('member', 'lev'), 'tile', 'row'), parts along dimension 0
- merid_out: float32 [128, 512, 512], P(('member', 'lev'), 'tile', 'row'), parts along dimension 0
There are 2 independent parts, one for each index of `member`. A program takes and returns all parts, laid end to end along the dimension named above; each array names one. Nothing has to cross between parts.
All inputs are finite; a program needn't handle non-finite values.
Results may differ from a plain program's by a relative error of at most 0.0003.
Values sent between devices are 32-bit elements; how exact they have to be, the bound alone decides.
A program may use at most 64 MiB of HBM per device.

v0:
```python
import jax
import jax.numpy as jnp
from jax import lax
from jax.sharding import PartitionSpec as P

NSUB = 4
CFL_NUMBER = 0.8


def one_axis_at_a_time(shard, axes):
    for axis in axes:
        shard = lax.pmax(shard, axis)
    return shard


def over_axes(shard, axes):
    for axis in axes:
        shard = lax.psum(shard, axis)
    return shard


def padded(block, sides, width):
    for axis, dim in sides:
        count = lax.axis_size(axis)
        forward = [(i, i + 1) for i in range(count - 1)]
        forward.append((count - 1, 0))
        backward = [(target, source) for source, target in forward]
        low = lax.ppermute(
            lax.slice_in_dim(block, block.shape[dim] - width, None, axis=dim), axis, forward
        )
        high = lax.ppermute(lax.slice_in_dim(block, 0, width, axis=dim), axis, backward)
        block = jnp.concatenate([low, block, high], axis=dim)
    return block


def joined_along(pieces, dim):
    pieces = jnp.moveaxis(pieces, 0, dim)
    dims = pieces.shape
    return pieces.reshape(*dims[:dim], dims[dim] * dims[dim + 1], *dims[dim + 2 :])


def sent_to_all(shard, axis):
    length = lax.axis_size(axis)
    return lax.all_to_all(
        jnp.broadcast_to(shard[None], (length, *shard.shape)), axis, 0, 0, tiled=True
    )


def gathered_copies(shard, axis, dim):
    return joined_along(sent_to_all(shard, axis), dim)


def advance(stacked, half_step):
    height = stacked[0]
    zonal = stacked[1]
    merid = stacked[2]
    zonal_new = zonal[:, 1:-1, 1:-1] - half_step * (height[:, 2:, 1:-1] - height[:, :-2, 1:-1])
    merid_new = merid[:, 1:-1, 1:-1] - half_step * (height[:, 1:-1, 2:] - height[:, 1:-1, :-2])
    centre = height[:, 1:-1, 1:-1]
    flux_east = centre * zonal_new
    flux_north = centre * merid_new
    height_new = centre[:, 1:-1, 1:-1] - half_step * (
        flux_east[:, 2:, 1:-1]
        - flux_east[:, :-2, 1:-1]
        + (flux_north[:, 1:-1, 2:] - flux_north[:, 1:-1, :-2])
    )
    return jnp.stack([height_new, zonal_new[:, 1:-1, 1:-1], merid_new[:, 1:-1, 1:-1]])


def remap_columns(columns, first, count):
    height = columns[0]
    zonal = columns[1]
    merid = columns[2]
    levels = height.shape[0]
    total = jnp.sum(height, 0)
    tops = jnp.cumsum(height, 0) - height
    marks = (first + jnp.arange(count + 1)).astype(jnp.float32)
    targets = total[None] * (marks / levels)[:, None, None]
    zonal_sum = jnp.zeros(targets.shape, jnp.float32)
    merid_sum = jnp.zeros(targets.shape, jnp.float32)
    for block in range(levels // 8):
        lower = block * 8
        upper = lower + 8
        over = jnp.clip(targets[None] - tops[lower:upper, None], 0.0, height[lower:upper, None])
        zonal_sum = zonal_sum + jnp.sum(zonal[lower:upper, None] * over, 0)
        merid_sum = merid_sum + jnp.sum(merid[lower:upper, None] * over, 0)
    layer = total / levels
    thick_new = jnp.broadcast_to(layer, (count,) + layer.shape)
    zonal_new = (zonal_sum[1:] - zonal_sum[:-1]) / layer
    merid_new = (merid_sum[1:] - merid_sum[:-1]) / layer
    return jnp.stack([thick_new, zonal_new, merid_new])


def local(thickness, zonal_wind, merid_wind, pert_codes):
    bump = 2.0 * (pert_codes % 4096).astype(jnp.float32) / 4095.0
    raised = thickness + bump[None]
    local_peak = jnp.max(raised)
    base_mass = jnp.sum(thickness)
    raised_mass = jnp.sum(raised)
    peak = one_axis_at_a_time(local_peak, ("tile", "row", "lev"))
    base_total, raised_total = (
        over_axes(base_mass, ("tile", "row", "lev")),
        over_axes(raised_mass, ("tile", "row", "lev")),
    )
    height = raised * (base_total / raised_total)
    half_step = 0.5 * CFL_NUMBER / jnp.sqrt(peak)
    state = jnp.stack([height, zonal_wind, merid_wind])
    state = padded(state, (("tile", 2), ("row", 3)), 2 * NSUB)
    for substep in range(NSUB):
        state = advance(state, half_step)
    levels_here = state.shape[1]
    columns = gathered_copies(state, "lev", 1)
    result = remap_columns(columns, lax.axis_index("lev") * levels_here, levels_here)
    return (result[0], result[1], result[2])


def solution(mesh):
    in_specs = (
        P(("member", "lev"), "tile", "row"),
        P(("member", "lev"), "tile", "row"),
        P(("member", "lev"), "tile", "row"),
        P(("member", "tile"), "row"),
    )
    out_specs = (
        P(("member", "lev"), "tile", "row"),
        P(("member", "lev"), "tile", "row"),
        P(("member", "lev"), "tile", "row"),
    )
    return jax.shard_map(local, mesh=mesh, in_specs=in_specs, out_specs=out_specs, check_vma=False)
```

profile of v0, /device:TPU:33, one launch (start us, length us, event | category | flops | bytes accessed | tf_op | source)
XLA Modules:
  0.0 252.3 jit_solution(18031665177296941275)
XLA Ops:
  1.4 1.6 add_reduce_fusion
  3.0 83.6 %all-reduce = (f32[]{:T(128)}, f32[]{:T(128)}) all-reduce(f32[]{:T(128)} %get-tuple-element.33, f32[]{:T(128)} %get-tuple-element.32), channel_id=1, replica_groups=mesh['member'=2,'tile'=32,'row'=4,'lev'=2] {'tile'}, use_global_device_ids=true, to_apply=%region_1.2 | all-reduce | flops 2 | bytes 16 | tf_op jit(solution)/shard_map/psum | solution.py:18
  86.7 9.5 %all-reduce.1 = (f32[]{:T(128)}, f32[]{:T(128)}) all-reduce(f32[]{:T(128)} %get-tuple-element.34, f32[]{:T(128)} %get-tuple-element.35), channel_id=1, replica_groups=mesh['member'=2,'tile'=32,'row'=4,'lev'=2] {'row'}, use_global_device_ids=true, to_apply=%region_2.3 | all-reduce | flops 2 | bytes 16 | tf_op jit(solution)/shard_map/psum | solution.py:18
  96.2 19.4 %all-reduce.2 = (f32[]{:T(128)}, f32[]{:T(128)}) all-reduce(f32[]{:T(128)} %get-tuple-element.36, f32[]{:T(128)} %get-tuple-element.37), channel_id=1, replica_groups=mesh['member'=2,'tile'=32,'row'=4,'lev'=2] {'lev'}, use_global_device_ids=true, to_apply=%region_3.4 | all-reduce | flops 2 | bytes 16 | tf_op jit(solution)/shard_map/psum | solution.py:18
  119.0 2.0 collective-permute-start
  121.0 4.6 %collective-permute-start.1 = (f32[3,32,8,128]{3,2,1,0:T(8,128)S(1)}, f32[3,32,8,128]{3,2,1,0:T(8,128)}, u32[]{:S(2)}, u32[]{:S(2)}) collective-permute-start(f32[3,32,8,128]{3,2,1,0:T(8,128)S(1)} %get-tuple-element.74), channel_id=1, source_target_pairs={{8,0},{16,8},{24,16},{32,24},{40,32},{48,40},{56,48},{64,56},{72,6... | collective-permute-start | bytes 1179656 | tf_op jit(solution)/shard_map/ppermute | solution.py:31
  125.6 46.2 %pmax.21 = f32[]{:T(128)} all-reduce(f32[]{:T(128)} %get-tuple-element.31), channel_id=1, replica_groups=mesh['member'=2,'tile'=32,'row'=4,'lev'=2] {'tile'}, use_global_device_ids=true, to_apply=%region_9.10 | all-reduce | flops 1 | bytes 8 | tf_op jit(solution)/shard_map/pmax | solution.py:12
  171.8 6.7 %pmax.22 = f32[]{:T(128)} all-reduce(f32[]{:T(128)} %pmax.21), channel_id=1, replica_groups=mesh['member'=2,'tile'=32,'row'=4,'lev'=2] {'row'}, use_global_device_ids=true, to_apply=%region_10.11 | all-reduce | flops 1 | bytes 8 | tf_op jit(solution)/shard_map/pmax | solution.py:12
  178.5 18.6 %pmax.23 = f32[]{:T(128)} all-reduce(f32[]{:T(128)} %pmax.22), channel_id=1, replica_groups=mesh['member'=2,'tile'=32,'row'=4,'lev'=2] {'lev'}, use_global_device_ids=true, to_apply=%region_11.12 | all-reduce | flops 1 | bytes 8 | tf_op jit(solution)/shard_map/pmax | solution.py:12
  197.8 1.3 pad_maximum_fusion.1
  200.9 3.6 %collective-permute-start.2 = (f32[3,32,32,8]{2,3,1,0:T(8,128)}, f32[3,32,32,8]{2,3,1,0:T(8,128)S(1)}, u32[]{:S(2)}, u32[]{:S(2)}) collective-permute-start(f32[3,32,32,8]{2,3,1,0:T(8,128)} %copy.20), channel_id=1, source_target_pairs={{0,2},{2,4},{4,6},{6,0},{1,3},{3,5},{5,7},{7,1},{8,10},{10,12},{12... | collective-permute-start | bytes 294920 | tf_op jit(solution)/shard_map/ppermute | solution.py:28
  205.0 3.1 %collective-permute-start.3 = (f32[3,32,32,8]{2,3,1,0:T(8,128)S(1)}, f32[3,32,32,8]{2,3,1,0:T(8,128)}, u32[]{:S(2)}, u32[]{:S(2)}) collective-permute-start(f32[3,32,32,8]{2,3,1,0:T(8,128)S(1)} %copy.21), channel_id=1, source_target_pairs={{2,0},{4,2},{6,4},{0,6},{3,1},{5,3},{7,5},{1,7},{10,8},{12,10},{14... | collective-permute-start | bytes 294920 | tf_op jit(solution)/shard_map/ppermute | solution.py:31
  208.1 6.5 %collective-permute-done.2 = f32[3,32,32,8]{2,3,1,0:T(8,128)S(1)} collective-permute-done((f32[3,32,32,8]{2,3,1,0:T(8,128)}, f32[3,32,32,8]{2,3,1,0:T(8,128)S(1)}, u32[]{:S(2)}, u32[]{:S(2)}) %collective-permute-start.2) | collective-permute-done | bytes 98336 | tf_op jit(solution)/shard_map/ppermute | solution.py:28
  215.1 2.0 collective-permute-done.3
  217.1 1.5 copy.19
  218.6 2.6 %pad_maximum_fusion = f32[3,32,32,144]{3,2,1,0:T(8,128)S(1)} fusion(f32[3,32,32,8]{3,2,1,0:T(8,128)S(1)} %copy.19, f32[3,32,8,128]{3,2,1,0:T(8,128)} %collective-permute-done.1, f32[1,32,16,128]{3,2,1,0:T(8,128)} %bitcast.26, f32[1,32,16,128]{3,2,1,0:T(8,128)} %bitcast.29, f32[1,32,16,128]{3,2,1,0:T(8,128)S(1)} %multiply_bitcast_fusion, ...), kind=kLoop, calls=%fused_computation | loop fusion | flops 2654208 | bytes 3538944 | tf_op jit(solution)/shard_map/concatenate | solution.py:32
  221.5 1.7 slice_multiply_fusion.3
  224.4 1.7 slice_multiply_fusion.1
  227.0 1.3 slice_multiply_fusion.7
  229.2 1.3 slice_multiply_fusion.5
  231.3 6.2 %all_to_all.5 = f32[2,3,32,16,128]{4,3,2,1,0:T(8,128)S(1)} all-to-all(f32[2,3,32,16,128]{4,3,2,1,0:T(8,128)S(1)} %broadcast_in_dim.2), channel_id=1, replica_groups=mesh['member'=2,'tile'=32,'row'=4,'lev'=2] {'lev'}, dimensions={0} | all-to-all | bytes 3145728 | tf_op jit(solution)/shard_map/all_to_all | solution.py:44
  237.7 6.9 %bitcast_subtract_fusion = f32[64,16,128]{2,1,0:T(8,128)S(1)} fusion(f32[1,2,32,16,128]{4,3,2,0,1:T(8,128)S(1)} %get-tuple-element.62, f32[64,16,128]{2,1,0:T(8,128)S(1)} %bitcast.22), kind=kOutput, calls=%fused_computation.104 | output fusion | flops 8388608 | bytes 1572864 | tf_op jit(solution)/shard_map/jit(cumsum)/reduce_window_sum | solution.py:76
  245.0 2.7 %multiply_reduce_fusion.7 = (f32[33,16,128]{2,1,0:T(8,128)S(1)}, f32[33,16,128]{2,1,0:T(8,128)S(1)}, f32[33,16,128]{2,1,0:T(8,128)S(1)}, f32[33,16,128]{2,1,0:T(...) fusion(f32[8,16,128]{2,1,0:T(8,128)S(1)} %get-tuple-element.82,, ...), kind=kLoop, calls=%fused_computation.8 | loop fusion | flops 14598144 | bytes 3481600 | tf_op jit(solution)/shard_map/reduce_sum | solution.py:86
  247.6 2.7 %multiply_reduce_fusion.6 = (f32[33,16,128]{2,1,0:T(8,128)S(1)}, f32[33,16,128]{2,1,0:T(8,128)S(1)}, f32[33,16,128]{2,1,0:T(8,128)S(1)}, f32[33,16,128]{2,1,0:T(...) fusion(f32[8,16,128]{2,1,0:T(8,128)S(1)} %get-tuple-element.81,, ...), kind=kLoop, calls=%fused_computation.7 | loop fusion | flops 14598144 | bytes 3481600 | tf_op jit(solution)/shard_map/reduce_sum | solution.py:86
  (34 shorter events, 12.2 us)
Async XLA Ops:
  0.6 197.2 %copy-start.1 = (f32[32,16,128]{2,1,0:T(8,128)S(1)}, f32[32,16,128]{2,1,0:T(8,128)}, u32[]{:S(2)}) copy-start(f32[32,16,128]{2,1,0:T(8,128)} %param.5) | copy-start | bytes 786436
  0.6 197.2 %copy-start = (f32[32,16,128]{2,1,0:T(8,128)S(1)}, f32[32,16,128]{2,1,0:T(8,128)}, u32[]{:S(2)}) copy-start(f32[32,16,128]{2,1,0:T(8,128)} %param.6) | copy-start | bytes 786436
  119.0 78.7 %collective-permute-start = (f32[3,32,8,128]{3,2,1,0:T(8,128)S(1)}, f32[3,32,8,128]{3,2,1,0:T(8,128)}, u32[]{:S(2)}, u32[]{:S(2)}) collective-permute-start(f32[3,32,8,128]{3,2,1,0:T(8,128)S(1)} %get-tuple-element.73), channel_id=1, source_target_pairs={{0,8},{8,16},{16,24},{24,32},{32,40},{40,48},{48,56},{56,64},{64,7... | collective-permute-start | bytes 1179656 | tf_op jit(solution)/shard_map/ppermute | solution.py:28
  121.0 76.8 %collective-permute-start.1 = (f32[3,32,8,128]{3,2,1,0:T(8,128)S(1)}, f32[3,32,8,128]{3,2,1,0:T(8,128)}, u32[]{:S(2)}, u32[]{:S(2)}) collective-permute-start(f32[3,32,8,128]{3,2,1,0:T(8,128)S(1)} %get-tuple-element.74), channel_id=1, source_target_pairs={{8,0},{16,8},{24,16},{32,24},{40,32},{48,40},{56,48},{64,56},{72,6... | collective-permute-start | bytes 1179656 | tf_op jit(solution)/shard_map/ppermute | solution.py:31
  200.9 13.7 %collective-permute-start.2 = (f32[3,32,32,8]{2,3,1,0:T(8,128)}, f32[3,32,32,8]{2,3,1,0:T(8,128)S(1)}, u32[]{:S(2)}, u32[]{:S(2)}) collective-permute-start(f32[3,32,32,8]{2,3,1,0:T(8,128)} %copy.20), channel_id=1, source_target_pairs={{0,2},{2,4},{4,6},{6,0},{1,3},{3,5},{5,7},{7,1},{8,10},{10,12},{12... | collective-permute-start | bytes 294920 | tf_op jit(solution)/shard_map/ppermute | solution.py:28
  205.0 12.1 %collective-permute-start.3 = (f32[3,32,32,8]{2,3,1,0:T(8,128)S(1)}, f32[3,32,32,8]{2,3,1,0:T(8,128)}, u32[]{:S(2)}, u32[]{:S(2)}) collective-permute-start(f32[3,32,32,8]{2,3,1,0:T(8,128)S(1)} %copy.21), channel_id=1, source_target_pairs={{2,0},{4,2},{6,4},{0,6},{3,1},{5,3},{7,5},{1,7},{10,8},{12,10},{14... | collective-permute-start | bytes 294920 | tf_op jit(solution)/shard_map/ppermute | solution.py:31
where the time goes:
time: 253 us; the launch traced here: 252 us
  blocking collectives  190 us (75%)
  other arithmetic  31.5 us (12%)
  starting transfers between devices  13.3 us (5%)
  waiting for transfers between devices  8.47 us (3%)
  local copies, waits for them, and re-layouts  5.87 us (2%)
  between operations  2.96 us (1%)
    psum x3, blocking collectives, over_axes(): shard = lax.psum(shard, axis)  113 us
    pmax x3, blocking collectives, one_axis_at_a_time(): shard = lax.pmax(shard, axis)  71.5 us
    ppermute x2, starting transfers between devices, padded(): lax.ppermute(lax.slice_in_dim(block, 0, width, axis=dim), axis, backward)  7.7 us
    another operation x1, other arithmetic, remap_columns(): tops = jnp.cumsum(height, 0) - height  6.88 us
    ppermute x2, waiting for transfers between devices, padded(): lax.ppermute(lax.slice_in_dim(block, block.shape[dim] - width, None, axis...  6.46 us
    all_to_all x1, blocking collectives, sent_to_all(): lax.all_to_all(jnp.broadcast_to(shard[None], (length, *shard.shape)), axi...  6.23 us
    mul x4, other arithmetic, advance(): flux_east = centre * zonal_new  5.99 us
    ppermute x2, starting transfers between devices, padded(): lax.ppermute(lax.slice_in_dim(block, block.shape[dim] - width, None, axis...  5.58 us
  transfers between devices with their start and end apart: 4, of which 2 were waited for; matrix products, arithmetic and copies ran while one was open for 0% of the time, Pallas kernels for 0%

commit v1 on v0

--- a/solution.py
+++ b/solution.py
@@ -15,7 +15,8 @@
 
 def over_axes(shard, axes):
     for axis in axes:
-        shard = lax.psum(shard, axis)
+        parts = lax.all_gather(shard, axis)
+        shard = jnp.sum(parts, axis=0)
     return shard
 
 

time: 253 us -> 269 us (1.063)
  local copies, waits for them, and re-layouts: 5.87 us -> 18.2 us
  other arithmetic: 31.5 us -> 35.2 us
  waiting for transfers between devices: 8.47 us -> 11.3 us
    psum x3 -> x0, blocking collectives: 113 us -> none  [over_axes(): shard = lax.psum(shard, axis)]
    unnamed x0 -> x3, blocking collectives: none -> 111 us
    unnamed x6 -> x21, local copies, waits for them, and re-layouts: 1.71 us -> 14 us
    ppermute x2, waiting for transfers between devices: 6.46 us -> 11.2 us  [padded(): lax.ppermute(lax.slice_in_dim(block, block.shape[dim] - width, None, axis...]
    reduce_sum x0 -> x6, other arithmetic: none -> 3.69 us  [over_axes(): shard = jnp.sum(parts, axis=0)]
  transfers between devices with their start and end apart: 4 -> 4, of which waited for: 2 -> 1; matrix products, arithmetic and copies ran while one was open for 0% -> 0% of each run, Pallas kernels for 0% -> 0%
where the time goes in v1:
time: 269 us; the launch traced here: 268 us
  blocking collectives  188 us (70%)
  other arithmetic  35.2 us (13%)
  local copies, waits for them, and re-layouts  18.2 us (7%)
  starting transfers between devices  12.3 us (5%)
  waiting for transfers between devices  11.3 us (4%)
  between operations  2.98 us (1%)
    unnamed x3, blocking collectives  111 us
    pmax x3, blocking collectives, one_axis_at_a_time(): shard = lax.pmax(shard, axis)  71.5 us
    unnamed x21, local copies, waits for them, and re-layouts  14 us
    ppermute x2, waiting for transfers between devices, padded(): lax.ppermute(lax.slice_in_dim(block, block.shape[dim] - width, None, axis...  11.2 us
    ppermute x2, starting transfers between devices, padded(): lax.ppermute(lax.slice_in_dim(block, 0, width, axis=dim), axis, backward)  8.25 us
    another operation x1, other arithmetic, remap_columns(): tops = jnp.cumsum(height, 0) - height  6.88 us
    all_to_all x1, blocking collectives, sent_to_all(): lax.all_to_all(jnp.broadcast_to(shard[None], (length, *shard.shape)), axi...  6.23 us
    mul x4, other arithmetic, advance(): flux_east = centre * zonal_new  5.99 us
  transfers between devices with their start and end apart: 4, of which 1 were waited for; matrix products, arithmetic and copies ran while one was open for 0% of the time, Pallas kernels for 0%

profile of v1, /device:TPU:33, one launch (start us, length us, event | category | flops | bytes accessed | tf_op | source)
XLA Modules:
  0.0 268.2 jit_solution(2638225719243329102)
XLA Ops:
  4.0 1.6 add_reduce_fusion
  8.3 83.0 %all-reduce.6 = (f32[32]{0:T(128)S(1)}, f32[32]{0:T(128)S(1)}) all-reduce(f32[32]{0:T(128)S(1)} %dynamic-update-slice, f32[32]{0:T(128)S(1)} %dynamic-update-slice.3), channel_id=1, replica_groups=mesh['member'=2,'tile'=32,'row'=4,'lev'=2] {'tile'}, use_global_device_ids=true, to_apply=%add | all-reduce | flops 64 | bytes 512
  92.5 1.4 dynamic-update-slice.4
  93.9 1.4 dynamic-update-slice.1
  96.6 8.9 %all-reduce.7 = (f32[4]{0:T(128)S(1)}, f32[4]{0:T(128)S(1)}) all-reduce(f32[4]{0:T(128)S(1)} %dynamic-update-slice.1, f32[4]{0:T(128)S(1)} %dynamic-update-slice.4), channel_id=1, replica_groups=mesh['member'=2,'tile'=32,'row'=4,'lev'=2] {'row'}, use_global_device_ids=true, to_apply=%add.1 | all-reduce | flops 8 | bytes 64
  106.8 1.4 dynamic-update-slice.5
  108.2 1.4 dynamic-update-slice.2
  109.6 18.8 %all-reduce.8 = (f32[2]{0:T(128)S(1)}, f32[2]{0:T(128)S(1)}) all-reduce(f32[2]{0:T(128)S(1)} %dynamic-update-slice.2, f32[2]{0:T(128)S(1)} %dynamic-update-slice.5), channel_id=1, replica_groups=mesh['member'=2,'tile'=32,'row'=4,'lev'=2] {'lev'}, use_global_device_ids=true, to_apply=%add.2 | all-reduce | flops 4 | bytes 32
  133.1 2.0 collective-permute-start
  135.0 4.6 %collective-permute-start.1 = (f32[3,32,8,128]{3,2,1,0:T(8,128)S(1)}, f32[3,32,8,128]{3,2,1,0:T(8,128)}, u32[]{:S(2)}, u32[]{:S(2)}) collective-permute-start(f32[3,32,8,128]{3,2,1,0:T(8,128)S(1)} %get-tuple-element.74), channel_id=1, source_target_pairs={{8,0},{16,8},{24,16},{32,24},{40,32},{48,40},{56,48},{64,56},{72,6... | collective-permute-start | bytes 1179656 | tf_op jit(solution)/shard_map/ppermute | solution.py:32
  139.6 46.2 %pmax.21 = f32[]{:T(128)} all-reduce(f32[]{:T(128)} %get-tuple-element.31), channel_id=1, replica_groups=mesh['member'=2,'tile'=32,'row'=4,'lev'=2] {'tile'}, use_global_device_ids=true, to_apply=%region_9.10 | all-reduce | flops 1 | bytes 8 | tf_op jit(solution)/shard_map/pmax | solution.py:12
  185.9 6.7 %pmax.22 = f32[]{:T(128)} all-reduce(f32[]{:T(128)} %pmax.21), channel_id=1, replica_groups=mesh['member'=2,'tile'=32,'row'=4,'lev'=2] {'row'}, use_global_device_ids=true, to_apply=%region_10.11 | all-reduce | flops 1 | bytes 8 | tf_op jit(solution)/shard_map/pmax | solution.py:12
  192.5 18.6 %pmax.23 = f32[]{:T(128)} all-reduce(f32[]{:T(128)} %pmax.22), channel_id=1, replica_groups=mesh['member'=2,'tile'=32,'row'=4,'lev'=2] {'lev'}, use_global_device_ids=true, to_apply=%region_11.12 | all-reduce | flops 1 | bytes 8 | tf_op jit(solution)/shard_map/pmax | solution.py:12
  215.4 3.6 %collective-permute-start.3 = (f32[3,32,32,8]{2,3,1,0:T(8,128)S(1)}, f32[3,32,32,8]{2,3,1,0:T(8,128)}, u32[]{:S(2)}, u32[]{:S(2)}) collective-permute-start(f32[3,32,32,8]{2,3,1,0:T(8,128)S(1)} %copy.21), channel_id=1, source_target_pairs={{2,0},{4,2},{6,4},{0,6},{3,1},{5,3},{7,5},{1,7},{10,8},{12,10},{14... | collective-permute-start | bytes 294920 | tf_op jit(solution)/shard_map/ppermute | solution.py:32
  219.0 2.1 collective-permute-start.2
  221.2 11.2 %collective-permute-done.2 = f32[3,32,32,8]{2,3,1,0:T(8,128)S(1)} collective-permute-done((f32[3,32,32,8]{2,3,1,0:T(8,128)}, f32[3,32,32,8]{2,3,1,0:T(8,128)S(1)}, u32[]{:S(2)}, u32[]{:S(2)}) %collective-permute-start.2) | collective-permute-done | bytes 98336 | tf_op jit(solution)/shard_map/ppermute | solution.py:29
  232.9 1.5 copy.19
  234.4 2.6 pad_maximum_fusion
  237.3 1.7 slice_multiply_fusion.3
  240.2 1.7 slice_multiply_fusion.1
  247.2 6.2 %all_to_all.5 = f32[2,3,32,16,128]{4,3,2,1,0:T(8,128)S(1)} all-to-all(f32[2,3,32,16,128]{4,3,2,1,0:T(8,128)S(1)} %broadcast_in_dim.2), channel_id=1, replica_groups=mesh['member'=2,'tile'=32,'row'=4,'lev'=2] {'lev'}, dimensions={0} | all-to-all | bytes 3145728 | tf_op jit(solution)/shard_map/all_to_all | solution.py:45
  253.6 6.9 %bitcast_subtract_fusion = f32[64,16,128]{2,1,0:T(8,128)S(1)} fusion(f32[1,2,32,16,128]{4,3,2,0,1:T(8,128)S(1)} %get-tuple-element.62, f32[64,16,128]{2,1,0:T(8,128)S(1)} %bitcast.31), kind=kOutput, calls=%fused_computation.104 | output fusion | flops 8388608 | bytes 1572864 | tf_op jit(solution)/shard_map/jit(cumsum)/reduce_window_sum | solution.py:77
  260.8 2.8 %multiply_reduce_fusion.7 = (f32[33,16,128]{2,1,0:T(8,128)S(1)}, f32[33,16,128]{2,1,0:T(8,128)S(1)}, f32[33,16,128]{2,1,0:T(8,128)S(1)}, f32[33,16,128]{2,1,0:T(...) fusion(f32[8,16,128]{2,1,0:T(8,128)S(1)} %get-tuple-element.82,, ...), kind=kLoop, calls=%fused_computation.8 | loop fusion | flops 14598144 | bytes 3481600 | tf_op jit(solution)/shard_map/reduce_sum | solution.py:87
  263.6 2.7 %multiply_reduce_fusion.6 = (f32[33,16,128]{2,1,0:T(8,128)S(1)}, f32[33,16,128]{2,1,0:T(8,128)S(1)}, f32[33,16,128]{2,1,0:T(8,128)S(1)}, f32[33,16,128]{2,1,0:T(...) fusion(f32[8,16,128]{2,1,0:T(8,128)S(1)} %get-tuple-element.81,, ...), kind=kLoop, calls=%fused_computation.7 | loop fusion | flops 14598144 | bytes 3481600 | tf_op jit(solution)/shard_map/reduce_sum | solution.py:87
  (55 shorter events, 26.2 us)
Async XLA Ops:
  0.6 211.2 %copy-start = (f32[32,16,128]{2,1,0:T(8,128)S(1)}, f32[32,16,128]{2,1,0:T(8,128)}, u32[]{:S(2)}) copy-start(f32[32,16,128]{2,1,0:T(8,128)} %param.6) | copy-start | bytes 786436
  0.6 211.2 %copy-start.1 = (f32[32,16,128]{2,1,0:T(8,128)S(1)}, f32[32,16,128]{2,1,0:T(8,128)}, u32[]{:S(2)}) copy-start(f32[32,16,128]{2,1,0:T(8,128)} %param.5) | copy-start | bytes 786436
  133.1 78.7 %collective-permute-start = (f32[3,32,8,128]{3,2,1,0:T(8,128)S(1)}, f32[3,32,8,128]{3,2,1,0:T(8,128)}, u32[]{:S(2)}, u32[]{:S(2)}) collective-permute-start(f32[3,32,8,128]{3,2,1,0:T(8,128)S(1)} %get-tuple-element.73), channel_id=1, source_target_pairs={{0,8},{8,16},{16,24},{24,32},{32,40},{40,48},{48,56},{56,64},{64,7... | collective-permute-start | bytes 1179656 | tf_op jit(solution)/shard_map/ppermute | solution.py:29
  135.0 76.8 %collective-permute-start.1 = (f32[3,32,8,128]{3,2,1,0:T(8,128)S(1)}, f32[3,32,8,128]{3,2,1,0:T(8,128)}, u32[]{:S(2)}, u32[]{:S(2)}) collective-permute-start(f32[3,32,8,128]{3,2,1,0:T(8,128)S(1)} %get-tuple-element.74), channel_id=1, source_target_pairs={{8,0},{16,8},{24,16},{32,24},{40,32},{48,40},{56,48},{64,56},{72,6... | collective-permute-start | bytes 1179656 | tf_op jit(solution)/shard_map/ppermute | solution.py:32
  215.4 17.5 %collective-permute-start.3 = (f32[3,32,32,8]{2,3,1,0:T(8,128)S(1)}, f32[3,32,32,8]{2,3,1,0:T(8,128)}, u32[]{:S(2)}, u32[]{:S(2)}) collective-permute-start(f32[3,32,32,8]{2,3,1,0:T(8,128)S(1)} %copy.21), channel_id=1, source_target_pairs={{2,0},{4,2},{6,4},{0,6},{3,1},{5,3},{7,5},{1,7},{10,8},{12,10},{14... | collective-permute-start | bytes 294920 | tf_op jit(solution)/shard_map/ppermute | solution.py:32
  219.0 13.4 %collective-permute-start.2 = (f32[3,32,32,8]{2,3,1,0:T(8,128)}, f32[3,32,32,8]{2,3,1,0:T(8,128)S(1)}, u32[]{:S(2)}, u32[]{:S(2)}) collective-permute-start(f32[3,32,32,8]{2,3,1,0:T(8,128)} %copy.20), channel_id=1, source_target_pairs={{0,2},{2,4},{4,6},{6,0},{1,3},{3,5},{5,7},{7,1},{8,10},{10,12},{12... | collective-permute-start | bytes 294920 | tf_op jit(solution)/shard_map/ppermute | solution.py:29
